TPU v7x, 32 devices: a whole 2x2x4 slice. The times are simulated.
32 devices in a mesh: space: 16 (over z, y, core), tensor: 2 (over x).
Axes of the slice: x: 2, y: 2, z: 4, core: 2. Of those that a mesh axis runs over, the one named last changes fastest.
Arguments:
- tokens: bfloat16 [14336, 1024], P('space', 'tensor'), may hold values from -6 to 6
- first_weight: bfloat16 [1024, 1024], P(None, 'tensor'), may hold values from -0.1875 to 0.1875
- second_weight: bfloat16 [1024, 1024], P(None, 'tensor'), may hold values from -0.1875 to 0.1875
- head_weight: bfloat16 [352, 1024], P('tensor'), may hold values from -0.1875 to 0.1875
- targets: float32 [352, 14336], P('tensor', 'space'), may hold values from -6 to 6
- land_mask: int32 [4, 14336], P(None, 'space'), may hold values from 0 to 1, as said below
- variable_kind: int32 [88], P('tensor'), may hold values from 0 to 2
- loss_scale: float32 [], replicated, may hold values from 630784 to 5046272
Outputs:
- loss: float32 [], replicated
- token_grad: float32 [14336, 1024], P('space', 'tensor')
- first_grad: float32 [1024, 1024], P('space', 'tensor')
- second_grad: float32 [1024, 1024], P('space', 'tensor')
- head_grad: float32 [352, 1024], P('tensor', 'space')
Inputs may be any that keep to these rules, and one draw needn't show every extreme that they name: `land_mask`: every aligned group of 8 entries along the last dimension holds at least one 1 and one 0. `variable_kind`: 0 scores a variable on all cells, 1 on land cells, 2 on ocean cells.
All inputs are finite; a program needn't handle non-finite values.
Results may differ from a plain program's by a relative error of at most 0.0056.
Values may be sent and summed in bfloat16 or wider, within the bound.
A program may use at most 64 MiB of HBM per device.

v0:
```python
import math
import jax
import jax.numpy as jnp
from jax import lax
from jax.sharding import PartitionSpec as P

V = 88
PP = 4
PROW_DEV = 4
LONP = 224


def slope(z):
    cdf = 0.5 * (1.0 + lax.erf(z / math.sqrt(2.0)))
    return cdf + z * jnp.exp(-0.5 * z * z) / math.sqrt(2.0 * math.pi)


def column_folder(weights, piece):
    return lax.dot_general(
        piece, weights, (((1,), (1,)), ((), ())), preferred_element_type=jnp.float32
    )


def row_folder(weights, piece):
    return lax.dot_general(
        piece, weights, (((0,), (0,)), ((), ())), preferred_element_type=jnp.float32
    )


def per_device(
    tokens, first_weight, second_weight, head_weight, targets, land_mask, variable_kind, loss_scale
):
    count = tokens.shape[0]
    width = first_weight.shape[1]
    kinds = head_weight.shape[0] // PP
    rows_first, rows_second = (
        lax.all_to_all(first_weight, "tensor", split_axis=0, concat_axis=1, tiled=True),
        lax.all_to_all(second_weight, "tensor", split_axis=0, concat_axis=1, tiled=True),
    )
    head_cols = lax.all_to_all(head_weight, "tensor", split_axis=1, concat_axis=0, tiled=True)
    position = lax.axis_index("space") * count + jnp.arange(count, dtype=jnp.int32)
    cell = jnp.arange(PP, dtype=jnp.int32)
    lat_row = 2 * (position // LONP)[None, :] + (cell // 2)[:, None]
    nlat = 2 * PROW_DEV * lax.axis_size("space")
    cell_weight = jnp.cos(math.pi / 2.0 * (lat_row.astype(jnp.float32) + 0.5) / nlat)
    land = land_mask.astype(jnp.float32)
    kind = variable_kind[:, None, None]
    valid = jnp.where(kind == 0, 1.0, jnp.where(kind == 1, land[None], 1.0 - land[None]))
    masked = cell_weight[None] * valid
    local_weight = jnp.sum(masked, axis=(1, 2))
    weight_sum = lax.psum(local_weight, "space")
    full_in = lax.all_gather(tokens, "tensor", axis=1, tiled=True)
    pre_one = jnp.dot(full_in, first_weight, preferred_element_type=jnp.float32)
    hidden_one = jax.nn.gelu(pre_one, approximate=False).astype(jnp.bfloat16)
    full_one = lax.all_gather(hidden_one, "tensor", axis=1, tiled=True)
    pre_two = jnp.dot(full_one, second_weight, preferred_element_type=jnp.float32)
    hidden_two = jax.nn.gelu(pre_two, approximate=False).astype(jnp.bfloat16)
    full_two = lax.all_gather(hidden_two, "tensor", axis=1, tiled=True)
    predicted = lax.dot_general(
        head_weight, full_two, (((1,), (1,)), ((), ())), preferred_element_type=jnp.float32
    )
    error = predicted.reshape(kinds, PP, count) - targets.reshape(kinds, PP, count)
    local_error = jnp.sum(masked * error * error, axis=(1, 2))
    error_sum = lax.psum(local_error, "space")
    root = jnp.sqrt(error_sum / weight_sum + 1e-06)
    loss = lax.psum(jnp.sum(root), "tensor") / V
    coef = loss_scale / (V * root * weight_sum)
    grad_pred = (
        (coef[:, None, None] * masked * error).reshape(kinds * PP, count).astype(jnp.bfloat16)
    )
    back_two = row_folder(head_cols, lax.all_gather(grad_pred, "tensor", axis=0, tiled=True))
    head_term = jnp.dot(grad_pred, full_two, preferred_element_type=jnp.float32)
    head_grad = lax.psum_scatter(head_term, "space", scatter_dimension=1, tiled=True)
    grad_two = (back_two * slope(pre_two)).astype(jnp.bfloat16)
    back_one = column_folder(rows_second, lax.all_gather(grad_two, "tensor", axis=1, tiled=True))
    grad_one = (back_one * slope(pre_one)).astype(jnp.bfloat16)
    joined = lax.psum_scatter(
        jnp.concatenate(
            [
                lax.dot_general(
                    full_one, grad_two, (((0,), (0,)), ((), ())), preferred_element_type=jnp.float32
                ),
                lax.dot_general(
                    full_in, grad_one, (((0,), (0,)), ((), ())), preferred_element_type=jnp.float32
                ),
            ],
            axis=1,
        ),
        "space",
        scatter_dimension=0,
        tiled=True,
    )
    second_grad = joined[:, :width]
    first_grad = joined[:, width:]
    token_grad = column_folder(rows_first, lax.all_gather(grad_one, "tensor", axis=1, tiled=True))
    return (loss, token_grad, first_grad, second_grad, head_grad)


def solution(mesh):
    return jax.shard_map(
        per_device,
        mesh=mesh,
        in_specs=(
            P("space", "tensor"),
            P(None, "tensor"),
            P(None, "tensor"),
            P("tensor", None),
            P("tensor", "space"),
            P(None, "space"),
            P("tensor"),
            P(),
        ),
        out_specs=(
            P(),
            P("space", "tensor"),
            P("space", "tensor"),
            P("space", "tensor"),
            P("tensor", "space"),
        ),
        check_vma=False,
    )
```

profile of v0, /device:TPU:0, one launch (start us, length us, event | category | flops | bytes accessed | tf_op | source)
XLA Modules:
  0.0 390.4 jit_solution(11387166332372937541)
XLA Ops:
  7.2 0.7 all-gather.6.cloned.1.call-update
  8.0 34.5 %all-gather.6.cloned.1.call-done = bf16[896,1024]{1,0:T(8,128)(2,1)} async-done(((bf16[896,512]{1,0:T(8,128)(2,1)}), bf16[896,1024]{1,0:T(8,128)(2,1)}) %all-gather.6.cloned.1.call-update) | async-done | bytes 1835024 | tf_op jit(solution)/shard_map/all_gather | solution.py:52
  42.4 8.0 %fusion.2 = (bf16[896,512]{1,0:T(8,128)(2,1)}, f32[896,512]{1,0:T(8,128)}) fusion(bf16[896,1024]{1,0:T(8,128)(2,1)} %all-gather.6.cloned.1.call-done, bf16[1024,512]{1,0:T(8,128)(2,1)} %param.9), kind=kOutput, calls=%fused_computation.7 | convolution fusion | flops 969342976 | bytes 5636096 | tf_op jit(solution)/shard_map/dot_general | solution.py:53
  50.5 30.2 %all-gather.8.cloned.1.call-done = bf16[896,1024]{1,0:T(8,128)(2,1)} async-done(((bf16[896,512]{1,0:T(8,128)(2,1)}), bf16[896,1024]{1,0:T(8,128)(2,1)}) %all-gather.8.cloned.1.call-update) | async-done | bytes 1835024 | tf_op jit(solution)/shard_map/all_gather | solution.py:55
  80.7 7.5 %fusion.5 = (bf16[896,512]{1,0:T(8,128)(2,1)}, f32[896,512]{1,0:T(8,128)}) fusion(bf16[896,1024]{1,0:T(8,128)(2,1)} %all-gather.8.cloned.1.call-done, bf16[1024,512]{1,0:T(8,128)(2,1)S(1)} %copy-done.4), kind=kOutput, calls=%fused_computation.10 | convolution fusion | flops 969342976 | bytes 5636096 | tf_op jit(solution)/shard_map/dot_general | solution.py:56
  88.2 0.8 copy.33
  89.0 4.2 %all-to-all-start = ((bf16[176,2,512]{2,0,1:T(8,128)(2,1)}), bf16[176,2,512]{2,0,1:T(8,128)(2,1)}, u32[]{:S(2)}, u32[]{:S(2)}) async-start(bf16[176,2,512]{2,0,1:T(8,128)(2,1)} %bitcast.37), calls=%async_computation | async-start | bytes 720896 | tf_op jit(solution)/shard_map/all_to_all | solution.py:40
  93.6 0.2 mul.117
  95.5 0.8 multiply_reduce_fusion
  96.3 23.1 %all-gather.10.cloned.1.call-done = bf16[896,1024]{1,0:T(8,128)(2,1)} async-done(((bf16[896,512]{1,0:T(8,128)(2,1)}), bf16[896,1024]{1,0:T(8,128)(2,1)}) %all-gather.10.cloned.1.call-update) | async-done | bytes 1835024 | tf_op jit(solution)/shard_map/all_gather | solution.py:58
  119.4 2.6 fusion.33
  122.2 33.2 %all-reduce = (f32[44]{0:T(128)S(1)}, f32[44]{0:T(128)S(1)}) all-reduce(f32[44]{0:T(128)S(1)} %reduce_sum.36, f32[44]{0:T(128)S(1)} %multiply_reduce_fusion), channel_id=1, replica_groups=mesh['space'=16,'tensor'=2] {'space'}, use_global_device_ids=true, to_apply=%region_2.3 | all-reduce | flops 88 | bytes 704 | tf_op jit(solution)/shard_map/psum | solution.py:64
  155.8 7.6 %all_gather.21 = bf16[352,896]{1,0:T(8,128)(2,1)S(1)} all-gather(bf16[176,896]{1,0:T(8,128)(2,1)S(1)} %multiply_convert_fusion), channel_id=1, replica_groups=mesh['space'=16,'tensor'=2] {'tensor'}, dimensions={0}, use_global_device_ids=true | all-gather | bytes 946176 | tf_op jit(solution)/shard_map/all_gather | solution.py:71
  163.4 3.7 fusion.11
  167.2 22.7 %all_to_all.57 = bf16[2,512,512]{2,1,0:T(8,128)(2,1)S(1)} all-to-all(bf16[2,512,512]{2,1,0:T(8,128)(2,1)S(1)} %bitcast.41), channel_id=1, replica_groups=mesh['space'=16,'tensor'=2] {'tensor'}, dimensions={0} | all-to-all | bytes 2097152 | tf_op jit(solution)/shard_map/all_to_all | solution.py:38
  189.9 0.5 copy.23
  190.4 8.6 %all-gather.12.cloned.1.call-done = bf16[896,1024]{1,0:T(8,128)(2,1)} async-done(((bf16[896,512]{1,0:T(8,128)(2,1)}), bf16[896,1024]{1,0:T(8,128)(2,1)}) %all-gather.12.cloned.1.call-update) | async-done | bytes 1835024 | tf_op jit(solution)/shard_map/all_gather | solution.py:75
  199.0 4.6 %fusion.17 = bf16[896,512]{1,0:T(8,128)(2,1)} fusion(f32[896,512]{1,0:T(8,128)} %get-tuple-element.36, bf16[896,1024]{1,0:T(8,128)(2,1)} %all-gather.12.cloned.1.call-done, bf16[512,1024]{0,1:T(8,128)(2,1)S(1)} %bitcast.44), kind=kOutput, calls=%fused_computation.22 | convolution fusion | flops 944111616 | bytes 5636096 | tf_op jit(solution)/shard_map/dot_general | solution.py:19
  203.7 3.2 fusion.38
  206.8 1.3 convolution_bitcast_fusion
  208.1 2.5 pad_maximum_fusion
  210.6 5.5 %copy.27 = f32[1024,1024]{1,0:T(8,128)} copy(f32[1024,1024]{0,1:T(8,128)} %pad_maximum_fusion) | data formatting | bytes 8388608
  216.2 3.7 all-to-all-start.2
  220.0 1.9 fusion.39
  221.9 0.6 reduce_sum.38
  222.5 22.4 %all-to-all-done.2 = bf16[2,512,512]{2,1,0:T(8,128)(2,1)S(1)} async-done(((bf16[2,512,512]{2,1,0:T(8,128)(2,1)}), bf16[2,512,512]{2,1,0:T(8,128)(2,1)S(1)}, u32[]{:S(2)}, u32[]{:S(2)}) %all-to-all-start.2) | async-done | bytes 1048608 | tf_op jit(solution)/shard_map/all_to_all | solution.py:37
  244.9 0.5 copy.24
  245.4 5.6 %psum.23 = f32[]{:T(128)} all-reduce(f32[]{:T(128)} %reduce_sum.38), channel_id=1, replica_groups=mesh['space'=16,'tensor'=2] {'tensor'}, use_global_device_ids=true, to_apply=%region_6.7 | all-reduce | flops 1 | bytes 8 | tf_op jit(solution)/shard_map/psum | solution.py:66
  251.7 3.9 fusion.37
  255.5 66.0 %reduce-scatter.7.cloned.1.call-done = f32[64,1024]{1,0:T(8,128)} async-done(((f32[1024,1024]{1,0:T(8,128)}), f32[64,1024]{1,0:T(8,128)}) %reduce-scatter.7.cloned.1.call-update) | async-done | bytes 262160
  321.5 1.7 fusion.36
  323.2 59.2 %reduce-scatter.5.cloned.1.call-done = f32[176,64]{0,1:T(8,128)} async-done(((f32[176,1024]{0,1:T(8,128)}), f32[176,64]{0,1:T(8,128)}) %reduce-scatter.5.cloned.1.call-update) | async-done | bytes 45072 | tf_op jit(solution)/shard_map/reduce_scatter | solution.py:73
  (51 shorter events, 2.3 us)
Async XLA Ops:
  7.2 35.2 %all-gather.6.cloned.1.call-start = ((), (), s32[]{:S(2)}) async-start(), calls=%async_computation.5 | async-start | bytes 2752512 | tf_op jit(solution)/shard_map/all_gather | solution.py:52
  7.9 72.8 %copy-start.4 = (bf16[1024,512]{1,0:T(8,128)(2,1)S(1)}, bf16[1024,512]{1,0:T(8,128)(2,1)}, u32[]{:S(2)}) copy-start(bf16[1024,512]{1,0:T(8,128)(2,1)} %param.10) | copy-start | bytes 3145732
  7.9 72.8 %all-gather.8.cloned.1.call-start = ((), (), s32[]{:S(2)}) async-start(), calls=%async_computation.6 | async-start | bytes 2752512 | tf_op jit(solution)/shard_map/all_gather | solution.py:55
  50.4 37.8 %copy-start.3 = (bf16[176,1024]{1,0:T(8,128)(2,1)S(1)}, bf16[176,1024]{1,0:T(8,128)(2,1)}, u32[]{:S(2)}) copy-start(bf16[176,1024]{1,0:T(8,128)(2,1)} %param.11) | copy-start | bytes 1081348
  50.4 69.0 %all-gather.10.cloned.1.call-start = ((), (), s32[]{:S(2)}) async-start(), calls=%async_computation.7 | async-start | bytes 2752512 | tf_op jit(solution)/shard_map/all_gather | solution.py:58
  88.2 5.0 %copy-start.6 = (s32[4,896]{1,0:T(4,128)S(1)}, s32[4,896]{1,0:T(4,128)}, u32[]{:S(2)}) copy-start(s32[4,896]{1,0:T(4,128)} %param.13) | copy-start | bytes 43012
  89.0 74.4 %all-to-all-start = ((bf16[176,2,512]{2,0,1:T(8,128)(2,1)}), bf16[176,2,512]{2,0,1:T(8,128)(2,1)}, u32[]{:S(2)}, u32[]{:S(2)}) async-start(bf16[176,2,512]{2,0,1:T(8,128)(2,1)} %bitcast.37), calls=%async_computation | async-start | bytes 720896 | tf_op jit(solution)/shard_map/all_to_all | solution.py:40
  93.2 105.8 %all-gather.12.cloned.1.call-start = ((), (), s32[]{:S(2)}) async-start(), calls=%async_computation.8 | async-start | bytes 2752512 | tf_op jit(solution)/shard_map/all_gather | solution.py:75
  93.8 0.7 copy-start.7
  163.4 3.8 copy-start.5
  167.2 84.5 %all-gather.14.cloned.1.call-start = ((), (), s32[]{:S(2)}) async-start(), calls=%async_computation.9 | async-start | bytes 2752512 | tf_op jit(solution)/shard_map/all_gather | solution.py:95
  203.6 3.2 copy-start.1
  203.6 3.2 copy-start.2
  203.6 117.9 %reduce-scatter.7.cloned.1.call-start = ((), (), s32[]{:S(2)}) async-start(), calls=%async_computation.11 | async-start | bytes 4456448
  216.2 3.8 copy-start
  216.2 28.7 %all-to-all-start.2 = ((bf16[2,512,512]{2,1,0:T(8,128)(2,1)}), bf16[2,512,512]{2,1,0:T(8,128)(2,1)S(1)}, u32[]{:S(2)}, u32[]{:S(2)}) async-start(bf16[2,512,512]{2,1,0:T(8,128)(2,1)} %bitcast.42), calls=%async_computation.2 | async-start | bytes 2097152 | tf_op jit(solution)/shard_map/all_to_all | solution.py:37
  219.9 162.5 %reduce-scatter.5.cloned.1.call-start = ((), (), s32[]{:S(2)}) async-start(), calls=%async_computation.10 | async-start | bytes 1114112 | tf_op jit(solution)/shard_map/reduce_scatter | solution.py:73
Sparse Core Ops, SparseCore 0:
  9.5 32.8 all-gather.5
  50.5 30.1 all-gather.7
  88.3 31.0 all-gather.9
  167.3 31.6 all-gather.11
  203.7 40.9 all-gather.13
  248.5 72.9 reduce-scatter.6
  325.7 56.6 reduce-scatter.4
where the time goes:
time: 391 us; the launch traced here: 390 us
  waiting for transfers between devices  245 us (63%)
  blocking collectives  69.1 us (18%)
  matrix products  36.5 us (9%)
  between operations  16.8 us (4%)
  local copies, waits for them, and re-layouts  10.7 us (3%)
  starting transfers between devices  8.16 us (2%)
  other arithmetic  4.37 us (1%)
    unnamed x8, waiting for transfers between devices  66.7 us
    reduce_scatter x1, waiting for transfers between devices, per_device(): lax.psum_scatter(head_term, 'space', scatter_dimension=1, tiled=True)  59.2 us
    all_gather x1, waiting for transfers between devices, per_device(): full_in = lax.all_gather(tokens, 'tensor', axis=1, tiled=True)  34.5 us
    psum x1, blocking collectives, per_device(): error_sum = lax.psum(local_error, 'space')  33.2 us
    all_gather x1, waiting for transfers between devices, per_device(): full_one = lax.all_gather(hidden_one, 'tensor', axis=1, tiled=True)  30.2 us
    all_gather x1, waiting for transfers between devices, per_device(): full_two = lax.all_gather(hidden_two, 'tensor', axis=1, tiled=True)  23.1 us
    all_to_all x1, blocking collectives, per_device(): lax.all_to_all(second_weight, 'tensor', split_axis=0, concat_axis=1, tile...  22.7 us
    all_to_all x1, waiting for transfers between devices, per_device(): lax.all_to_all(first_weight, 'tensor', split_axis=0, concat_axis=1, tiled...  22.4 us
  transfers between devices with their start and end apart: 9, of which 7 were waited for; matrix products, arithmetic and copies ran while one was open for 7% of the time, Pallas kernels for 0%

commit v1 on v0

--- a/solution.py
+++ b/solution.py
@@ -61,7 +61,11 @@
     )
     error = predicted.reshape(kinds, PP, count) - targets.reshape(kinds, PP, count)
     local_error = jnp.sum(masked * error * error, axis=(1, 2))
-    error_sum = lax.psum(local_error, "space")
+    error_sum = local_error
+    for hop in (1, 2, 4, 8):
+        error_sum = error_sum + lax.ppermute(
+            error_sum, "space", [(dev, dev ^ hop) for dev in range(16)]
+        )
     root = jnp.sqrt(error_sum / weight_sum + 1e-06)
     loss = lax.psum(jnp.sum(root), "tensor") / V
     coef = loss_scale / (V * root * weight_sum)

time: 391 us -> 404 us (1.033)
  waiting for transfers between devices: 245 us -> 250 us
  starting transfers between devices: 8.16 us -> 13 us
    all_gather x1, waiting for transfers between devices: 23.1 us -> 28.7 us  [per_device(): full_two = lax.all_gather(hidden_two, 'tensor', axis=1, tiled=True)]
    ppermute x0 -> x4, starting transfers between devices: none -> 5.51 us  [per_device(): lax.ppermute(error_sum, 'space', [(dev, dev ^ hop) for dev in range(16)])]
  transfers between devices with their start and end apart: 9 -> 13, of which waited for: 7 -> 9; matrix products, arithmetic and copies ran while one was open for 7% -> 6% of each run, Pallas kernels for 0% -> 0%
where the time goes in v1:
time: 404 us; the launch traced here: 403 us
  waiting for transfers between devices  250 us (62%)
  blocking collectives  71 us (18%)
  matrix products  37.1 us (9%)
  between operations  16.9 us (4%)
  starting transfers between devices  13 us (3%)
  local copies, waits for them, and re-layouts  10.5 us (3%)
  other arithmetic  4.39 us (1%)
    unnamed x8, waiting for transfers between devices  66.7 us
    reduce_scatter x1, waiting for transfers between devices, per_device(): lax.psum_scatter(head_term, 'space', scatter_dimension=1, tiled=True)  59.3 us
    all_gather x1, waiting for transfers between devices, per_device(): full_in = lax.all_gather(tokens, 'tensor', axis=1, tiled=True)  34.5 us
    all_gather x1, waiting for transfers between devices, per_device(): full_one = lax.all_gather(hidden_one, 'tensor', axis=1, tiled=True)  30.2 us
    psum x1, blocking collectives, per_device(): weight_sum = lax.psum(local_weight, 'space')  29.5 us
    all_gather x1, waiting for transfers between devices, per_device(): full_two = lax.all_gather(hidden_two, 'tensor', axis=1, tiled=True)  28.7 us
    all_to_all x1, blocking collectives, per_device(): lax.all_to_all(second_weight, 'tensor', split_axis=0, concat_axis=1, tile...  25.8 us
    all_to_all x1, waiting for transfers between devices, per_device(): lax.all_to_all(first_weight, 'tensor', split_axis=0, concat_axis=1, tiled...  19 us
  transfers between devices with their start and end apart: 13, of which 9 were waited for; matrix products, arithmetic and copies ran while one was open for 6% of the time, Pallas kernels for 0%

profile of v1, /device:TPU:0, one launch (start us, length us, event | category | flops | bytes accessed | tf_op | source)
XLA Modules:
  0.0 403.1 jit_solution(16856663475010830772)
XLA Ops:
  8.0 34.5 %all-gather.6.cloned.1.call-done = bf16[896,1024]{1,0:T(8,128)(2,1)} async-done(((bf16[896,512]{1,0:T(8,128)(2,1)}), bf16[896,1024]{1,0:T(8,128)(2,1)}) %all-gather.6.cloned.1.call-update) | async-done | bytes 1835024 | tf_op jit(solution)/shard_map/all_gather | solution.py:52
  42.4 8.0 %fusion.2 = (bf16[896,512]{1,0:T(8,128)(2,1)}, f32[896,512]{1,0:T(8,128)}) fusion(bf16[896,1024]{1,0:T(8,128)(2,1)} %all-gather.6.cloned.1.call-done, bf16[1024,512]{1,0:T(8,128)(2,1)} %param.9), kind=kOutput, calls=%fused_computation.7 | convolution fusion | flops 969342976 | bytes 5636096 | tf_op jit(solution)/shard_map/dot_general | solution.py:53
  50.5 30.2 %all-gather.8.cloned.1.call-done = bf16[896,1024]{1,0:T(8,128)(2,1)} async-done(((bf16[896,512]{1,0:T(8,128)(2,1)}), bf16[896,1024]{1,0:T(8,128)(2,1)}) %all-gather.8.cloned.1.call-update) | async-done | bytes 1835024 | tf_op jit(solution)/shard_map/all_gather | solution.py:55
  80.7 7.5 %fusion.5 = (bf16[896,512]{1,0:T(8,128)(2,1)}, f32[896,512]{1,0:T(8,128)}) fusion(bf16[896,1024]{1,0:T(8,128)(2,1)} %all-gather.8.cloned.1.call-done, bf16[1024,512]{1,0:T(8,128)(2,1)S(1)} %copy-done.5), kind=kOutput, calls=%fused_computation.10 | convolution fusion | flops 969342976 | bytes 5636096 | tf_op jit(solution)/shard_map/dot_general | solution.py:56
  89.8 28.7 %all-gather.10.cloned.1.call-done = bf16[896,1024]{1,0:T(8,128)(2,1)} async-done(((bf16[896,512]{1,0:T(8,128)(2,1)}), bf16[896,1024]{1,0:T(8,128)(2,1)}) %all-gather.10.cloned.1.call-update) | async-done | bytes 1835024 | tf_op jit(solution)/shard_map/all_gather | solution.py:58
  118.5 3.3 fusion.33
  122.1 1.1 collective-permute-done
  123.3 1.5 collective-permute-start.1
  124.7 0.8 copy.33
  125.5 3.5 all-to-all-start
  129.0 1.6 collective-permute-start.2
  130.6 0.8 multiply_reduce_fusion
  131.4 1.3 collective-permute-done.2
  132.7 2.4 collective-permute-start.3
  135.7 29.5 %psum.14 = f32[44]{0:T(128)S(1)} all-reduce(f32[44]{0:T(128)S(1)} %multiply_reduce_fusion), channel_id=1, replica_groups=mesh['space'=16,'tensor'=2] {'space'}, use_global_device_ids=true, to_apply=%region_3.4 | all-reduce | flops 44 | bytes 352 | tf_op jit(solution)/shard_map/psum | solution.py:51
  165.6 10.1 %all_gather.21 = bf16[352,896]{1,0:T(8,128)(2,1)S(1)} all-gather(bf16[176,896]{1,0:T(8,128)(2,1)S(1)} %multiply_convert_fusion), channel_id=1, replica_groups=mesh['space'=16,'tensor'=2] {'tensor'}, dimensions={0}, use_global_device_ids=true | all-gather | bytes 946176 | tf_op jit(solution)/shard_map/all_gather | solution.py:75
  175.7 3.6 fusion.11
  179.4 25.8 %all_to_all.57 = bf16[2,512,512]{2,1,0:T(8,128)(2,1)S(1)} all-to-all(bf16[2,512,512]{2,1,0:T(8,128)(2,1)S(1)} %bitcast.41), channel_id=1, replica_groups=mesh['space'=16,'tensor'=2] {'tensor'}, dimensions={0} | all-to-all | bytes 2097152 | tf_op jit(solution)/shard_map/all_to_all | solution.py:38
  205.8 9.4 %all-gather.12.cloned.1.call-done = bf16[896,1024]{1,0:T(8,128)(2,1)} async-done(((bf16[896,512]{1,0:T(8,128)(2,1)}), bf16[896,1024]{1,0:T(8,128)(2,1)}) %all-gather.12.cloned.1.call-update) | async-done | bytes 1835024 | tf_op jit(solution)/shard_map/all_gather | solution.py:79
  215.2 4.6 %fusion.17 = bf16[896,512]{1,0:T(8,128)(2,1)} fusion(f32[896,512]{1,0:T(8,128)} %get-tuple-element.34, bf16[896,1024]{1,0:T(8,128)(2,1)} %all-gather.12.cloned.1.call-done, bf16[512,1024]{0,1:T(8,128)(2,1)S(1)} %bitcast.44), kind=kOutput, calls=%fused_computation.22 | convolution fusion | flops 944111616 | bytes 5636096 | tf_op jit(solution)/shard_map/dot_general | solution.py:19
  219.9 3.2 fusion.38
  223.1 1.3 convolution_bitcast_fusion
  224.4 2.5 pad_maximum_fusion
  226.9 5.3 %copy.27 = f32[1024,1024]{1,0:T(8,128)} copy(f32[1024,1024]{0,1:T(8,128)} %pad_maximum_fusion) | data formatting | bytes 8388608
  232.3 3.7 all-to-all-start.2
  236.1 1.9 fusion.39
  238.6 19.0 %all-to-all-done.2 = bf16[2,512,512]{2,1,0:T(8,128)(2,1)S(1)} async-done(((bf16[2,512,512]{2,1,0:T(8,128)(2,1)}), bf16[2,512,512]{2,1,0:T(8,128)(2,1)S(1)}, u32[]{:S(2)}, u32[]{:S(2)}) %all-to-all-start.2) | async-done | bytes 1048608 | tf_op jit(solution)/shard_map/all_to_all | solution.py:37
  258.1 5.6 %psum.15 = f32[]{:T(128)} all-reduce(f32[]{:T(128)} %reduce_sum.38), channel_id=1, replica_groups=mesh['space'=16,'tensor'=2] {'tensor'}, use_global_device_ids=true, to_apply=%region_5.6 | all-reduce | flops 1 | bytes 8 | tf_op jit(solution)/shard_map/psum | solution.py:70
  264.4 3.9 fusion.37
  268.2 65.9 %reduce-scatter.7.cloned.1.call-done = f32[64,1024]{1,0:T(8,128)} async-done(((f32[1024,1024]{1,0:T(8,128)}), f32[64,1024]{1,0:T(8,128)}) %reduce-scatter.7.cloned.1.call-update) | async-done | bytes 262160
  334.2 1.7 fusion.36
  335.9 59.3 %reduce-scatter.5.cloned.1.call-done = f32[176,64]{0,1:T(8,128)} async-done(((f32[176,1024]{0,1:T(8,128)}), f32[176,64]{0,1:T(8,128)}) %reduce-scatter.5.cloned.1.call-update) | async-done | bytes 45072 | tf_op jit(solution)/shard_map/reduce_scatter | solution.py:77
  (64 shorter events, 5.0 us)
Async XLA Ops:
  7.2 35.2 %all-gather.6.cloned.1.call-start = ((), (), s32[]{:S(2)}) async-start(), calls=%async_computation.5 | async-start | bytes 2752512 | tf_op jit(solution)/shard_map/all_gather | solution.py:52
  7.9 72.8 %copy-start.5 = (bf16[1024,512]{1,0:T(8,128)(2,1)S(1)}, bf16[1024,512]{1,0:T(8,128)(2,1)}, u32[]{:S(2)}) copy-start(bf16[1024,512]{1,0:T(8,128)(2,1)} %param.10) | copy-start | bytes 3145732
  7.9 72.8 %all-gather.8.cloned.1.call-start = ((), (), s32[]{:S(2)}) async-start(), calls=%async_computation.6 | async-start | bytes 2752512 | tf_op jit(solution)/shard_map/all_gather | solution.py:55
  50.4 37.8 %copy-start.7 = (s32[4,896]{1,0:T(4,128)S(1)}, s32[4,896]{1,0:T(4,128)}, u32[]{:S(2)}) copy-start(s32[4,896]{1,0:T(4,128)} %param.13) | copy-start | bytes 43012
  50.4 68.1 %all-gather.10.cloned.1.call-start = ((), (), s32[]{:S(2)}) async-start(), calls=%async_computation.7 | async-start | bytes 2752512 | tf_op jit(solution)/shard_map/all_gather | solution.py:58
  88.4 0.7 copy-start.8
  88.8 29.7 %copy-start.4 = (bf16[176,1024]{1,0:T(8,128)(2,1)S(1)}, bf16[176,1024]{1,0:T(8,128)(2,1)}, u32[]{:S(2)}) copy-start(bf16[176,1024]{1,0:T(8,128)(2,1)} %param.11) | copy-start | bytes 1081348
  121.8 43.6 %copy-start.2 = (f32[176,896]{1,0:T(8,128)S(1)}, f32[176,896]{1,0:T(8,128)}, u32[]{:S(2)}) copy-start(f32[176,896]{1,0:T(8,128)} %get-tuple-element.37) | copy-start | bytes 1892356
  122.0 1.2 collective-permute-start
  123.3 5.8 %collective-permute-start.1 = (f32[44]{0:T(128)S(1)}, f32[44]{0:T(128)S(1)}, u32[]{:S(2)}, u32[]{:S(2)}) collective-permute-start(f32[44]{0:T(128)S(1)} %add.92), channel_id=1, source_target_pairs={{0,4},{2,6},{4,0},{6,2},{8,12},{10,14},{12,8},{14,10},{16,20},{18,... | collective-permute-start | bytes 536 | tf_op jit(solution)/shard_map/ppermute | solution.py:66
  125.5 50.2 %all-to-all-start = ((bf16[176,2,512]{2,0,1:T(8,128)(2,1)}), bf16[176,2,512]{2,0,1:T(8,128)(2,1)S(1)}, u32[]{:S(2)}, u32[]{:S(2)}) async-start(bf16[176,2,512]{2,0,1:T(8,128)(2,1)} %bitcast.37), calls=%async_computation | async-start | bytes 720896 | tf_op jit(solution)/shard_map/all_to_all | solution.py:40
  129.0 86.3 %all-gather.12.cloned.1.call-start = ((), (), s32[]{:S(2)}) async-start(), calls=%async_computation.8 | async-start | bytes 2752512 | tf_op jit(solution)/shard_map/all_gather | solution.py:79
  129.0 3.6 collective-permute-start.2
  132.7 32.6 %collective-permute-start.3 = (f32[44]{0:T(128)S(1)}, f32[44]{0:T(128)S(1)}, u32[]{:S(2)}, u32[]{:S(2)}) collective-permute-start(f32[44]{0:T(128)S(1)} %add.94), channel_id=1, source_target_pairs={{0,16},{2,18},{4,20},{6,22},{8,24},{10,26},{12,28},{14,30},{16,0},... | collective-permute-start | bytes 536 | tf_op jit(solution)/shard_map/ppermute | solution.py:66
  175.7 3.7 copy-start.6
  179.4 85.0 %all-gather.14.cloned.1.call-start = ((), (), s32[]{:S(2)}) async-start(), calls=%async_computation.9 | async-start | bytes 2752512 | tf_op jit(solution)/shard_map/all_gather | solution.py:99
  219.8 3.2 copy-start.1
  219.9 3.2 copy-start.3
  219.9 114.3 %reduce-scatter.7.cloned.1.call-start = ((), (), s32[]{:S(2)}) async-start(), calls=%async_computation.11 | async-start | bytes 4456448
  232.3 3.8 copy-start
  232.3 25.3 %all-to-all-start.2 = ((bf16[2,512,512]{2,1,0:T(8,128)(2,1)}), bf16[2,512,512]{2,1,0:T(8,128)(2,1)S(1)}, u32[]{:S(2)}, u32[]{:S(2)}) async-start(bf16[2,512,512]{2,1,0:T(8,128)(2,1)} %bitcast.42), calls=%async_computation.2 | async-start | bytes 2097152 | tf_op jit(solution)/shard_map/all_to_all | solution.py:37
  236.0 159.2 %reduce-scatter.5.cloned.1.call-start = ((), (), s32[]{:S(2)}) async-start(), calls=%async_computation.10 | async-start | bytes 1114112 | tf_op jit(solution)/shard_map/reduce_scatter | solution.py:77
Sparse Core Ops, SparseCore 0:
  9.5 32.8 all-gather.5
  50.5 30.1 all-gather.7
  88.3 30.1 all-gather.9
  179.5 35.6 all-gather.11
  220.0 34.1 all-gather.13
  257.8 76.2 reduce-scatter.6
  338.4 56.7 reduce-scatter.4
